TPU v7x, 256 devices: a whole 4x4x8 slice. The times are simulated.
256 devices in a mesh: seq: 32 (over y, z), head: 8 (over x, core).
Axes of the slice: x: 4, y: 4, z: 8, core: 2. Of those that a mesh axis runs over, the one named last changes fastest.
Arguments:
- tokens: bfloat16 [24576, 2560], P(('seq', 'head')), may hold values from -12 to 12
- pre_gain: float32 [2560], replicated, may hold values from 0.25 to 1.75
- inner_proj: bfloat16 [2560, 2, 5120], P(None, None, 'head'), may hold values from -0.125 to 0.125
- outer_proj: bfloat16 [2560, 336], replicated, may hold values from -0.125 to 0.125
- kernel_x: float32 [4, 5120], P(None, 'head'), may hold values from -3 to 3
- kernel_bc: float32 [4, 256], replicated, may hold values from -3 to 3
- offset_x: float32 [5120], P('head'), may hold values from -3 to 3
- offset_bc: float32 [256], replicated, may hold values from -3 to 3
- dt_bias: float32 [80], P('head'), may hold values from -7 to -5
- a_log: float32 [80], P('head'), may hold values from -12 to 4
- skip_gain: float32 [80], P('head'), may hold values from 0.5 to 1.5
- norm_gain: float32 [5120], P('head'), may hold values from 0.25 to 1.75
- out_proj: bfloat16 [5120, 2560], P('head'), may hold values from -0.078125 to 0.078125
Outputs:
- mixed: bfloat16 [24576, 2560], P(('seq', 'head'))
All inputs are finite; a program needn't handle non-finite values.
Results may differ from a plain program's by a relative error of at most 0.014.
Values may be sent and summed in bfloat16 or wider, within the bound.
A program may use at most 128 MiB of HBM per device.

v0:
```python
import jax
import jax.numpy as jnp
from jax import lax
from jax.sharding import Mesh
from jax.sharding import PartitionSpec as P

SPAN = 256
SEQ = ("seq_0", "seq_1")
SEQ_HEAD = ("seq_0", "seq_1", "head")
norm_floor = 0.1


def passed_along(block, axis, distance):
    devices = range(lax.axis_size(axis))
    route = [(i - distance, i) for i in devices if i - distance in devices]
    return lax.ppermute(block, axis, route)


def nothing_yet(array, identity):
    return jax.tree.map(
        lambda part, zero: jnp.zeros_like(part) + jnp.asarray(zero, part.dtype), array, identity
    )


def entering(array, axes, combine, identity):
    before = start = nothing_yet(array, identity)
    subtotal = array
    for axis in reversed(axes):
        length, position = (lax.axis_size(axis), lax.axis_index(axis))
        pieces = jax.tree.map(
            lambda part, kind: lax.all_gather(part.astype(kind), axis),
            subtotal,
            (jnp.bfloat16, jnp.bfloat16),
        )
        inside, subtotal = (start, start)
        for k in range(length):
            passed = k < position
            subtotal = combine(
                subtotal, jax.tree.map(lambda part, own: part[k].astype(own.dtype), pieces, array)
            )
            inside = jax.tree.map(lambda new, old: jnp.where(passed, new, old), subtotal, inside)
        before = combine(inside, before)
    return before


def from_everyone(array, axis):
    length = lax.axis_size(axis)
    return lax.all_to_all(
        jnp.broadcast_to(array[None], (length, *array.shape)), axis, 0, 0, tiled=True
    )


def taken_together(array, axis):
    everything = from_everyone(array, axis)
    return jnp.sum(everything, axis=0)


def cut_along(array, dim, length):
    before, after = (array.shape[:dim], array.shape[dim + 1 :])
    return jnp.moveaxis(array.reshape(*before, length, -1, *after), dim, 0)


def summed_on_arrival(array, axis, dim):
    pieces = cut_along(array, dim, lax.axis_size(axis))
    arrived = lax.all_to_all(pieces, axis, split_axis=0, concat_axis=0, tiled=True)
    return arrived.astype(jnp.float32).sum(axis=0)


def row_norm(row_block, gain_vector):
    widened = row_block.astype(jnp.float32)
    inverse_rms = lax.rsqrt(jnp.mean(widened * widened, axis=-1, keepdims=True) + norm_floor)
    return widened * inverse_rms * gain_vector


def masked_exp(log_gap, causal):
    return jnp.where(causal, jnp.exp(jnp.where(causal, log_gap, 0.0)), 0.0)


def on_device(
    tokens,
    pre_gain,
    inner_proj,
    outer_proj,
    kernel_x,
    kernel_bc,
    offset_x,
    offset_bc,
    dt_bias,
    a_log,
    skip_gain,
    norm_gain,
    out_proj,
):
    model_width = inner_proj.shape[0]
    local_width = inner_proj.shape[2]
    head_count = dt_bias.shape[0]
    head_size = local_width // head_count
    state_size = kernel_bc.shape[1] // 2
    kernel_size = kernel_x.shape[0]
    joined_proj = inner_proj.reshape(model_width, 2 * local_width)
    own_normed = row_norm(tokens, pre_gain).astype(jnp.bfloat16)
    normed = lax.all_gather(own_normed, "head", axis=0, tiled=True)
    inner_part = jnp.dot(normed, joined_proj, preferred_element_type=jnp.float32)
    outer_part = jnp.dot(normed, outer_proj, preferred_element_type=jnp.float32)
    projected = jnp.concatenate([inner_part, outer_part], axis=1)
    seq_rows = projected.shape[0]
    gate_in = projected[:, :local_width].astype(jnp.bfloat16)
    conv_input = projected[:, local_width : 2 * local_width + 2 * state_size].astype(jnp.bfloat16)
    head_index = lax.axis_index("head")
    dt_raw = lax.dynamic_slice_in_dim(
        projected[:, 2 * local_width + 2 * state_size :], head_index * head_count, head_count, 1
    )
    conv_tail = passed_along(conv_input[seq_rows - kernel_size + 1 :], SEQ, 1)
    extended = jnp.concatenate([conv_tail, conv_input], axis=0)
    conv_weight = jnp.concatenate([kernel_x, kernel_bc], axis=1)
    conv_bias = jnp.concatenate([offset_x, offset_bc])
    summed = jnp.broadcast_to(conv_bias, conv_input.shape)
    for offset in range(kernel_size):
        summed = summed + conv_weight[offset] * extended[offset : offset + seq_rows].astype(
            jnp.float32
        )
    conv_out = jax.nn.silu(summed).astype(jnp.bfloat16)
    blocks = seq_rows // SPAN
    values_x = conv_out[:, :local_width].reshape(blocks, SPAN, head_count, head_size)
    values_b = conv_out[:, local_width : local_width + state_size].reshape(blocks, SPAN, state_size)
    values_c = conv_out[:, local_width + state_size :].reshape(blocks, SPAN, state_size)
    step_flat = jax.nn.softplus(dt_raw + dt_bias)
    log_rates = (step_flat * -jnp.exp(a_log)).reshape(blocks, SPAN, head_count)
    step_sizes = step_flat.reshape(blocks, SPAN, head_count)
    running = jnp.cumsum(log_rates, axis=1)
    score_rows = jnp.einsum("ctn,csn->cts", values_c, values_b, preferred_element_type=jnp.float32)
    running_heads = jnp.transpose(running, (0, 2, 1))
    steps_heads = jnp.transpose(step_sizes, (0, 2, 1))
    row_index = lax.broadcasted_iota(jnp.int32, (SPAN, SPAN), 0)
    col_index = lax.broadcasted_iota(jnp.int32, (SPAN, SPAN), 1)
    decay_factor = masked_exp(
        running_heads[:, :, :, None] - running_heads[:, :, None, :], row_index >= col_index
    )
    mix_weights = (score_rows[:, None] * decay_factor * steps_heads[:, :, None, :]).astype(
        jnp.bfloat16
    )
    intra_out = jnp.einsum(
        "chts,cshp->cthp", mix_weights, values_x, preferred_element_type=jnp.float32
    )
    end_weight = jnp.exp(running[:, -1:, :] - running) * step_sizes
    scaled_x = (values_x.astype(jnp.float32) * end_weight[..., None]).astype(jnp.bfloat16)
    block_states = jnp.einsum(
        "cshp,csn->chpn", scaled_x, values_b, preferred_element_type=jnp.float32
    )
    block_total = running[:, -1, :]
    prefix_rate = jnp.concatenate(
        [jnp.zeros((1, head_count), jnp.float32), jnp.cumsum(block_total, axis=0)], axis=0
    )
    prefix_heads = prefix_rate.T
    later_index = lax.broadcasted_iota(jnp.int32, (blocks + 1, blocks), 0)
    source_index = lax.broadcasted_iota(jnp.int32, (blocks + 1, blocks), 1)
    link_weight = masked_exp(
        prefix_heads[:, :, None] - prefix_heads[:, None, 1:], source_index < later_index
    )
    local_states = jnp.einsum(
        "hce,ehpn->chpn", link_weight, block_states, precision=lax.Precision.HIGHEST
    )
    summary = local_states[blocks]
    device_rate = prefix_rate[blocks]

    def combine(earlier_part, later_part):
        return (
            earlier_part[0] + later_part[0],
            jnp.exp(later_part[0])[:, None, None] * earlier_part[1] + later_part[1],
        )

    identity = (
        jnp.zeros((head_count,), jnp.float32),
        jnp.zeros((head_count, head_size, state_size), jnp.float32),
    )
    carried = entering((device_rate, summary), SEQ, combine, identity)[1]
    block_inputs = (
        local_states[:blocks] + jnp.exp(prefix_rate[:blocks])[:, :, None, None] * carried[None]
    )
    cross_out = jnp.exp(running)[..., None] * jnp.einsum(
        "ctn,chpn->cthp",
        values_c.astype(jnp.float32),
        block_inputs,
        precision=lax.Precision.HIGHEST,
    )
    mixer_out = (intra_out + cross_out + skip_gain[:, None] * values_x.astype(jnp.float32)).reshape(
        seq_rows, local_width
    )
    gated = mixer_out * jax.nn.silu(gate_in.astype(jnp.float32))
    squares = taken_together(jnp.sum(gated * gated, axis=1), "head")
    inverse_rms = lax.rsqrt(squares / (local_width * lax.axis_size("head")) + norm_floor)
    normed_out = (gated * inverse_rms[:, None] * norm_gain).astype(jnp.bfloat16)
    mixed = summed_on_arrival(
        jnp.dot(normed_out, out_proj, preferred_element_type=jnp.float32).astype(jnp.bfloat16),
        "head",
        0,
    )
    return mixed.astype(jnp.bfloat16)


def solution(mesh):
    finer = Mesh(mesh.devices.reshape(4, 8, mesh.shape["head"]), ("seq_0", "seq_1", "head"))
    in_specs = (
        P(SEQ_HEAD, None),
        P(),
        P(None, None, "head"),
        P(),
        P(None, "head"),
        P(),
        P("head"),
        P(),
        P("head"),
        P("head"),
        P("head"),
        P("head"),
        P("head", None),
    )
    out_specs = P(SEQ_HEAD, None)
    return jax.shard_map(
        on_device, mesh=finer, in_specs=in_specs, out_specs=out_specs, check_vma=False
    )
```

profile of v0, /device:TPU:1, one launch (start us, length us, event | category | flops | bytes accessed | tf_op | source)
XLA Modules:
  0.0 240.8 jit_solution(7252940572213324971)
XLA Ops:
  6.5 1.4 fusion.16
  7.9 2.0 fusion.18
  10.1 6.7 %copy.137 = bf16[320,8,2,640]{3,1,2,0:T(8,128)(2,1)} copy(bf16[320,8,2,640]{3,2,1,0:T(2,128)(2,1)} %bitcast.167) | data formatting | bytes 13107200
  16.8 0.6 iota_compare_fusion.1
  17.4 0.6 pad_maximum_fusion.3
  18.1 29.7 %all-gather.5.cloned.1.call-done = bf16[768,2560]{1,0:T(8,128)(2,1)} async-done(((bf16[96,2560]{1,0:T(8,128)(2,1)}), bf16[768,2560]{1,0:T(8,128)(2,1)}) %all-gather.5.cloned.1.call-update) | async-done | bytes 3932176 | tf_op jit(solution)/shard_map/all_gather | solution.py:102
  47.8 5.3 %fusion.66 = (bf16[768,336]{0,1:T(8,128)(2,1)}, f32[768,336]{0,1:T(8,128)}) fusion(bf16[768,2560]{1,0:T(8,128)(2,1)} %all-gather.5.cloned.1.call-done, bf16[2560,336]{0,1:T(8,128)(2,1)} %param.16), kind=kOutput, calls=%fused_computation.144 | convolution fusion | flops 1321463808 | bytes 7200768 | tf_op jit(solution)/shard_map/dot_general | solution.py:104
  53.1 2.1 copy.111
  55.2 8.9 %convolution_convert_fusion.1 = bf16[768,1280]{1,0:T(8,128)(2,1)S(1)} fusion(bf16[768,2560]{1,0:T(8,128)(2,1)} %all-gather.5.cloned.1.call-done, bf16[2560,1280]{1,0:T(8,128)(2,1)} %bitcast.168), kind=kOutput, calls=%fused_computation.9 | convolution fusion | flops 5034147840 | bytes 12451840 | tf_op jit(solution)/shard_map/dot_general | solution.py:103
  64.2 1.3 pad_maximum_fusion.1
  65.5 0.4 copy-done.1
  65.9 0.6 pad_maximum_fusion.2
  66.5 1.0 slice.213
  67.4 0.1 broadcast_multiply_fusion
  67.6 1.7 reduce-window.6
  69.3 0.2 slice_reduce_fusion
  69.6 0.1 broadcast_add_fusion
  69.8 0.1 copy.121
  69.9 0.1 copy.122
  70.1 3.2 %collective-permute-start = (bf16[3,896]{1,0:T(4,128)(2,1)}, bf16[3,896]{1,0:T(4,128)(2,1)S(1)}, u32[]{:S(2)}, u32[]{:S(2)}) collective-permute-start(bf16[3,896]{1,0:T(4,128)(2,1)} %pad_maximum_fusion.2), channel_id=1, source_target_pairs={{0,8},{8,16},{16,24},{24,32},{32,40},{40,48},{48,56},{56,64},{64,7... | collective-permute-start | bytes 16136 | tf_op jit(solution)/shard_map/ppermute | solution.py:16
  73.3 0.6 bitcast_exponential_fusion
  73.9 0.7 copy.124
  74.6 0.6 copy.123
  75.2 0.7 copy.125
  75.9 5.0 %multiply_convert_fusion.2 = bf16[768,896]{1,0:T(8,128)(2,1)S(1)} fusion(bf16[768,896]{1,0:T(8,128)(2,1)} %pad_maximum_fusion.1, bf16[3,896]{1,0:T(4,128)(2,1)S(1)} %collective-permute-done, f32[896]{0:T(1024)S(1)} %get-tuple-element.6, f32[896]{0:T(1024)S(1)} %get-tuple-element.7, f32[896]{0:T(1024)S(1)} %get-tuple-element.8, f32[896]{0:T(1024)S(1)} %get-tuple-element.5, ...), kind=kLoop, calls=%fused_computation.10 | loop fusion | flops 17891328 | bytes 2775808 | tf_op jit(solution)/shard_map/convert_element_type | solution.py:122
  80.9 0.7 fusion.65
  81.6 1.1 slice.210
  82.6 2.3 copy.112
  84.9 3.8 %reshape.237 = bf16[3,256,10,64]{1,0,3,2:T(4,128)(2,1)} reshape(bf16[768,640]{0,1:T(8,128)(2,1)} %copy.112) | data formatting | bytes 1966080 | tf_op jit(solution)/shard_map/reshape | solution.py:124
  88.7 1.8 fusion.19
  90.5 2.8 %convolution_bitcast_fusion = f32[4,10,64,128]{3,0,2,1:T(4,128)S(1)} fusion(f32[3,10,64,128]{3,2,1,0:T(8,128)S(1)} %fusion.19, f32[10,3]{1,0:T(8,128)S(1)} %copy-done.14, f32[10,4]{1,0:T(8,128)S(1)} %copy-done.13, pred[4,3]{1,0:T(4,128)(4,1)S(1)} %copy-done.27), kind=kOutput, calls=%fused_computation.26 | convolution fusion | flops 11796840 | bytes 2294052 | tf_op jit(solution)/shard_map/hce,ehpn->chpn/dot_general | solution.py:160
  93.4 1.1 copy-done.2
  94.4 0.3 slice.387
  94.8 0.7 copy.128
  95.5 0.6 iota_compare_fusion
  96.2 1.4 slice_exponential_fusion
  97.5 12.2 %all-gather = bf16[8,1,10]{2,1,0:T(2,128)(2,1)S(1)} all-gather(bf16[1,1,10]{2,1,0:T(2,128)(2,1)S(1)} %slice_bitcast_fusion.5), channel_id=1, replica_groups=mesh['seq_0'=4,'seq_1'=8,'head'=8] {'seq_1'}, dimensions={0}, use_global_device_ids=true | all-gather | bytes 180 | tf_op jit(solution)/shard_map/all_gather | solution.py:31
  109.7 0.6 fusion.39
  110.3 0.6 convert_bitcast_fusion
  110.9 8.6 %all-gather.1 = bf16[4,1,10]{2,1,0:T(2,128)(2,1)} all-gather(bf16[1,1,10]{2,1,0:T(2,128)(2,1)S(1)} %get-tuple-element.17), channel_id=1, replica_groups=mesh['seq_0'=4,'seq_1'=8,'head'=8] {'seq_0'}, dimensions={0}, use_global_device_ids=true | all-gather | bytes 100 | tf_op jit(solution)/shard_map/all_gather | solution.py:31
  119.5 0.6 copy.115
  120.2 0.8 copy.127
  120.9 1.4 copy.119
  122.3 0.6 copy.117
  123.0 0.6 exponential_bitcast_fusion
  123.6 0.7 fusion.49
  124.3 2.1 fusion.67
  126.4 4.1 %all-gather.7.cloned.1.call-done = bf16[8,10,64,128]{3,2,1,0:T(8,128)(2,1)} async-done(((bf16[1,10,64,128]{3,2,1,0:T(8,128)(2,1)}), bf16[8,10,64,128]{3,2,1,0:T(8,128)(2,1)}) %all-gather.7.cloned.1.call-update) | async-done | bytes 1310736 | tf_op jit(solution)/shard_map/all_gather | solution.py:31
  130.4 1.9 fusion.28
  132.3 10.4 %all_gather.23 = bf16[4,10,64,128]{3,2,1,0:T(8,128)(2,1)S(1)} all-gather(bf16[1,10,64,128]{3,2,1,0:T(8,128)(2,1)S(1)} %fusion.28), channel_id=1, replica_groups=mesh['seq_0'=4,'seq_1'=8,'head'=8] {'seq_0'}, dimensions={0}, use_global_device_ids=true | all-gather | bytes 819200 | tf_op jit(solution)/shard_map/all_gather | solution.py:31
  142.8 1.0 add_bitcast_fusion
  143.8 0.4 slice_add_fusion
  144.3 0.9 fusion.21
  145.2 0.3 copy-done.6
  145.5 0.2 copy-done.7
  145.7 2.7 %fusion.8 = f32[3,256,10,64]{1,3,2,0:T(8,128)S(1)} fusion(f32[3,256,10,64]{1,3,2,0:T(8,128)S(1)} %fusion.21, f32[3,10,256]{2,1,0:T(8,128)S(1)} %copy-done.11, f32[3,10,256]{2,1,0:T(8,128)S(1)} %copy-done.9, f32[3,256,256]{2,1,0:T(8,128)S(1)} %copy-done.7, pred[256,256]{1,0:T(8,128)(4,1)S(1)} %copy-done.8, f32[10]{0:T(128)S(1)} %copy-done.30, ...), kind=kOutput, calls=%fused_computation.16 | convolution fusion | flops 265912320 | bytes 5859368 | tf_op jit(solution)/shard_map/chts,cshp->cthp/dot_general | solution.py:142
  148.4 1.4 copy.130
  149.8 1.8 copy.138
  151.6 2.8 %copy.131 = f32[768,640]{1,0:T(8,128)} copy(f32[768,640]{0,1:T(8,128)} %bitcast.166) | data formatting | bytes 3932160 | tf_op jit(solution)/shard_map/reshape | solution.py:186
  154.4 2.5 %multiply_reduce_fusion = f32[768]{0:T(1024)S(1)} fusion(f32[768,640]{1,0:T(8,128)} %copy.131, bf16[768,1280]{1,0:T(8,128)(2,1)} %copy-done.1), kind=kLoop, calls=%fused_computation.23 | loop fusion | flops 3931392 | bytes 2952192 | tf_op jit(solution)/shard_map/reduce_sum | solution.py:190
  156.9 17.4 %all_to_all.11 = f32[8,1,768]{2,1,0:T(1,128)S(1)} all-to-all(f32[8,1,768]{2,1,0:T(1,128)S(1)} %broadcast_in_dim.36), channel_id=1, replica_groups=mesh['seq_0'=4,'seq_1'=8,'head'=8] {'head'}, dimensions={0} | all-to-all | bytes 49152 | tf_op jit(solution)/shard_map/all_to_all | solution.py:48
  174.4 6.2 %convolution_convert_fusion = bf16[768,2560]{1,0:T(8,128)(2,1)S(1)} fusion(bf16[640,2560]{1,0:T(8,128)(2,1)S(1)} %copy-done, f32[640]{0:T(1024)S(1)} %copy-done.28, f32[768]{0:T(1024)S(1)} %add_rsqrt_fusion, f32[768,640]{1,0:T(8,128)} %copy.131, bf16[768,1280]{1,0:T(8,128)(2,1)} %copy-done.1), kind=kOutput, calls=%fused_computation.1 | convolution fusion | flops 2522972160 | bytes 10163712 | tf_op jit(solution)/shard_map/dot_general | solution.py:194
  180.6 49.8 %all_to_all.12 = bf16[8,96,2560]{2,1,0:T(8,128)(2,1)} all-to-all(bf16[8,96,2560]{2,1,0:T(8,128)(2,1)S(1)} %bitcast.169), channel_id=1, replica_groups=mesh['seq_0'=4,'seq_1'=8,'head'=8] {'head'}, dimensions={0} | all-to-all | bytes 7864320 | tf_op jit(solution)/shard_map/all_to_all | solution.py:65
  230.4 3.6 %reduce_sum.42 = bf16[96,2560]{1,0:T(8,128)(2,1)} reduce(bf16[8,96,2560]{2,1,0:T(8,128)(2,1)} %all_to_all.12, bf16[]{:T(256)} %constant.60.clone.1), dimensions={0}, to_apply=%region_6.7 | reduce | flops 1720320 | bytes 4423682 | tf_op jit(solution)/shard_map/reduce_sum | solution.py:66
  (84 shorter events, 0.6 us)
Async XLA Ops:
  6.5 167.9 %copy-start = (bf16[640,2560]{1,0:T(8,128)(2,1)S(1)}, bf16[640,2560]{1,0:T(8,128)(2,1)}, u32[]{:S(2)}) copy-start(bf16[640,2560]{1,0:T(8,128)(2,1)} %param.25) | copy-start | bytes 9830404
  6.5 41.2 %all-gather.5.cloned.1.call-start = ((), (), s32[]{:S(2)}) async-start(), calls=%async_computation.2 | async-start | bytes 4423680 | tf_op jit(solution)/shard_map/all_gather | solution.py:102
  10.0 120.5 %all-gather.7.cloned.1.call-start = ((), (), s32[]{:S(2)}) async-start(), calls=%async_computation.3 | async-start | bytes 1474560 | tf_op jit(solution)/shard_map/all_gather | solution.py:31
  10.0 7.4 %copy-start.16 = (f32[4,640]{1,0:T(4,128)S(1)}, f32[4,640]{1,0:T(4,128)}, u32[]{:S(2)}) copy-start(f32[4,640]{1,0:T(4,128)} %param.17) | copy-start | bytes 30724
  10.0 7.4 %copy-start.22 = (f32[4,256]{1,0:T(4,128)S(1)}, f32[4,256]{1,0:T(4,128)}, u32[]{:S(2)}) copy-start(f32[4,256]{1,0:T(4,128)} %param.18) | copy-start | bytes 12292
  10.0 7.4 %copy-start.23 = (f32[640]{0:T(1024)S(1)}, f32[640]{0:T(1024)}, u32[]{:S(2)}) copy-start(f32[640]{0:T(1024)} %param.19) | copy-start | bytes 7684
  10.1 7.4 %copy-start.25 = (f32[256]{0:T(256)S(1)}, f32[256]{0:T(256)}, u32[]{:S(2)}) copy-start(f32[256]{0:T(256)} %param.20) | copy-start | bytes 3076
  10.1 8.0 %copy-start.29 = (f32[10]{0:T(128)S(1)}, f32[10]{0:T(128)}, u32[]{:S(2)}) copy-start(f32[10]{0:T(128)} %param.22) | copy-start | bytes 124
  55.2 8.9 %copy-start.4 = (bf16[768,336]{1,0:T(8,128)(2,1)S(1)}, bf16[768,336]{1,0:T(8,128)(2,1)}, u32[]{:S(2)}) copy-start(bf16[768,336]{1,0:T(8,128)(2,1)} %copy.111) | copy-start | bytes 1548292
  64.2 1.7 copy-start.1
  65.9 1.6 copy-start.26
  70.0 5.9 %copy-start.15 = (f32[3,10]{1,0:T(4,128)}, f32[3,10]{1,0:T(4,128)S(1)}, u32[]{:S(2)}) copy-start(f32[3,10]{1,0:T(4,128)S(1)} %reduce_window_sum.36) | copy-start | bytes 364
  70.1 5.8 %collective-permute-start = (bf16[3,896]{1,0:T(4,128)(2,1)}, bf16[3,896]{1,0:T(4,128)(2,1)S(1)}, u32[]{:S(2)}, u32[]{:S(2)}) collective-permute-start(bf16[3,896]{1,0:T(4,128)(2,1)} %pad_maximum_fusion.2), channel_id=1, source_target_pairs={{0,8},{8,16},{16,24},{24,32},{32,40},{40,48},{48,56},{56,64},{64,7... | collective-permute-start | bytes 16136 | tf_op jit(solution)/shard_map/ppermute | solution.py:16
  88.7 1.8 copy-start.13
  88.7 1.8 copy-start.14
  88.7 1.8 copy-start.27
  93.4 1.1 copy-start.2
  109.7 10.4 %copy-start.12 = (bf16[8,1,10]{2,1,0:T(2,128)(2,1)}, bf16[8,1,10]{2,1,0:T(2,128)(2,1)S(1)}, u32[]{:S(2)}) copy-start(bf16[8,1,10]{2,1,0:T(2,128)(2,1)S(1)} %all-gather) | copy-start | bytes 484
  120.1 22.6 %copy-start.17 = (f32[10]{0:T(128)S(1)}, f32[10]{0:T(128)}, u32[]{:S(2)}) copy-start(f32[10]{0:T(128)} %get-tuple-element.18) | copy-start | bytes 124
  120.1 22.6 %copy-start.18 = (f32[10]{0:T(128)S(1)}, f32[10]{0:T(128)}, u32[]{:S(2)}) copy-start(f32[10]{0:T(128)} %get-tuple-element.19) | copy-start | bytes 124
  120.1 22.6 %copy-start.19 = (f32[10]{0:T(128)S(1)}, f32[10]{0:T(128)}, u32[]{:S(2)}) copy-start(f32[10]{0:T(128)} %get-tuple-element.20) | copy-start | bytes 124
  120.1 22.6 %copy-start.20 = (f32[10]{0:T(128)S(1)}, f32[10]{0:T(128)}, u32[]{:S(2)}) copy-start(f32[10]{0:T(128)} %get-tuple-element.21) | copy-start | bytes 124
  120.2 22.6 %copy-start.21 = (f32[10]{0:T(128)S(1)}, f32[10]{0:T(128)}, u32[]{:S(2)}) copy-start(f32[10]{0:T(128)} %get-tuple-element.22) | copy-start | bytes 124
  123.0 19.8 %copy-start.24 = (f32[10]{0:T(128)S(1)}, f32[10]{0:T(128)}, u32[]{:S(2)}) copy-start(f32[10]{0:T(128)} %get-tuple-element.9) | copy-start | bytes 124
  130.4 12.3 %copy-start.5 = (bf16[8,10,64,128]{3,2,1,0:T(8,128)(2,1)S(1)}, bf16[8,10,64,128]{3,2,1,0:T(8,128)(2,1)}, u32[]{:S(2)}) copy-start(bf16[8,10,64,128]{3,2,1,0:T(8,128)(2,1)} %all-gather.7.cloned.1.call-done) | copy-start | bytes 3932164
  130.4 13.3 %copy-start.3 = (f32[4,10,64,128]{3,0,2,1:T(4,128)S(1)}, f32[4,10,64,128]{3,0,2,1:T(4,128)}, u32[]{:S(2)}) copy-start(f32[4,10,64,128]{3,0,2,1:T(4,128)} %copy-done.2) | copy-start | bytes 3932164
  144.2 1.3 copy-start.6
  144.2 1.5 copy-start.7
  144.2 1.5 copy-start.8
  144.2 1.5 copy-start.9
  144.2 1.5 copy-start.10
  144.2 1.5 copy-start.11
  144.2 1.5 copy-start.30
  154.4 20.0 %copy-start.28 = (f32[640]{0:T(1024)S(1)}, f32[640]{0:T(1024)}, u32[]{:S(2)}) copy-start(f32[640]{0:T(1024)} %param.24) | copy-start | bytes 7684
Sparse Core Ops, SparseCore 0:
  10.1 37.6 all-gather.4
  95.6 34.7 all-gather.6
where the time goes:
time: 242 us; the launch traced here: 241 us
  blocking collectives  98.4 us (41%)
  waiting for transfers between devices  33.8 us (14%)
  local copies, waits for them, and re-layouts  32.7 us (14%)
  matrix products  30.8 us (13%)
  other arithmetic  28 us (12%)
  between operations  13.9 us (6%)
  starting transfers between devices  3.23 us (1%)
    all_to_all x1, blocking collectives, summed_on_arrival(): lax.all_to_all(pieces, axis, split_axis=0, concat_axis=0, tiled=True)  49.8 us
    all_gather x3, blocking collectives, entering(): lax.all_gather(part.astype(kind), axis)  31.2 us
    all_gather x1, waiting for transfers between devices, on_device(): normed = lax.all_gather(own_normed, 'head', axis=0, tiled=True)  29.7 us
    all_to_all x1, blocking collectives, from_everyone(): lax.all_to_all(jnp.broadcast_to(array[None], (length, *array.shape)), axi...  17.4 us
    unnamed x66, local copies, waits for them, and re-layouts  10.6 us
    dot_general x1, matrix products, on_device(): jnp.dot(normed, joined_proj, preferred_element_type=jnp.float32)  8.94 us
    dot_general x1, matrix products, on_device(): jnp.dot(normed_out, out_proj, preferred_element_type=jnp.float32)  6.16 us
    dot_general x1, matrix products, on_device(): outer_part = jnp.dot(normed, outer_proj, preferred_element_type=jnp.float32)  5.31 us
  transfers between devices with their start and end apart: 3, of which 2 were waited for; matrix products, arithmetic and copies ran while one was open for 9% of the time, Pallas kernels for 0%

commit v1 on v0

--- a/solution.py
+++ b/solution.py
@@ -99,7 +99,9 @@
     kernel_size = kernel_x.shape[0]
     joined_proj = inner_proj.reshape(model_width, 2 * local_width)
     own_normed = row_norm(tokens, pre_gain).astype(jnp.bfloat16)
-    normed = lax.all_gather(own_normed, "head", axis=0, tiled=True)
+    normed = jnp.concatenate(
+        lax.all_to_all(jnp.stack([own_normed] * lax.axis_size("head")), "head", 0, 0), axis=0
+    )
     inner_part = jnp.dot(normed, joined_proj, preferred_element_type=jnp.float32)
     outer_part = jnp.dot(normed, outer_proj, preferred_element_type=jnp.float32)
     projected = jnp.concatenate([inner_part, outer_part], axis=1)

time: 242 us -> 259 us (1.070)
  waiting for transfers between devices: 33.8 us -> 41.5 us
  starting transfers between devices: 3.23 us -> 9.62 us
    all_to_all x0 -> x1, waiting for transfers between devices: none -> 38 us  [on_device(): lax.all_to_all(jnp.stack([own_normed] * lax.axis_size('head')), 'head', 0...]
    all_gather x1 -> x0, waiting for transfers between devices: 29.7 us -> none  [on_device(): normed = lax.all_gather(own_normed, 'head', axis=0, tiled=True)]
    all_to_all x0 -> x1, starting transfers between devices: none -> 7.6 us  [on_device(): lax.all_to_all(jnp.stack([own_normed] * lax.axis_size('head')), 'head', 0...]
    unnamed x66 -> x68, local copies, waits for them, and re-layouts: 10.6 us -> 10.4 us
  transfers between devices with their start and end apart: 3 -> 3, of which waited for: 2 -> 2; matrix products, arithmetic and copies ran while one was open for 9% -> 8% of each run, Pallas kernels for 0% -> 0%
where the time goes in v1:
time: 259 us; the launch traced here: 258 us
  blocking collectives  100 us (39%)
  waiting for transfers between devices  41.5 us (16%)
  local copies, waits for them, and re-layouts  34.9 us (13%)
  matrix products  30 us (12%)
  other arithmetic  27.9 us (11%)
  between operations  13.9 us (5%)
  starting transfers between devices  9.62 us (4%)
    all_to_all x1, blocking collectives, summed_on_arrival(): lax.all_to_all(pieces, axis, split_axis=0, concat_axis=0, tiled=True)  49.8 us
    all_to_all x1, waiting for transfers between devices, on_device(): lax.all_to_all(jnp.stack([own_normed] * lax.axis_size('head')), 'head', 0...  38 us
    all_gather x3, blocking collectives, entering(): lax.all_gather(part.astype(kind), axis)  33.2 us
    all_to_all x1, blocking collectives, from_everyone(): lax.all_to_all(jnp.broadcast_to(array[None], (length, *array.shape)), axi...  17.4 us
    unnamed x68, local copies, waits for them, and re-layouts  10.4 us
    dot_general x1, matrix products, on_device(): jnp.dot(normed, joined_proj, preferred_element_type=jnp.float32)  7.94 us
    all_to_all x1, starting transfers between devices, on_device(): lax.all_to_all(jnp.stack([own_normed] * lax.axis_size('head')), 'head', 0...  7.6 us
    dot_general x1, matrix products, on_device(): jnp.dot(normed_out, out_proj, preferred_element_type=jnp.float32)  6.16 us
  transfers between devices with their start and end apart: 3, of which 2 were waited for; matrix products, arithmetic and copies ran while one was open for 8% of the time, Pallas kernels for 0%

profile of v1, /device:TPU:1, one launch (start us, length us, event | category | flops | bytes accessed | tf_op | source)
XLA Modules:
  0.0 258.2 jit_solution(9409515362096897362)
XLA Ops:
  6.5 1.4 fusion.16
  7.9 1.2 fusion.18
  9.2 2.3 stack.2
  11.5 7.6 %all-to-all-start = ((bf16[8,96,2560]{2,1,0:T(8,128)(2,1)}), bf16[8,96,2560]{2,1,0:T(8,128)(2,1)}, u32[]{:S(2)}, u32[]{:S(2)}) async-start(bf16[8,96,2560]{2,1,0:T(8,128)(2,1)} %stack.2), calls=%async_computation | async-start | bytes 7864320 | tf_op jit(solution)/shard_map/all_to_all | solution.py:103
  19.1 6.7 %copy.137 = bf16[320,8,2,640]{3,1,2,0:T(8,128)(2,1)} copy(bf16[320,8,2,640]{3,2,1,0:T(2,128)(2,1)} %bitcast.168) | data formatting | bytes 13107200
  25.9 0.5 iota_compare_fusion.1
  26.4 0.6 pad_maximum_fusion.3
  27.1 38.0 %all-to-all-done = bf16[8,96,2560]{2,1,0:T(8,128)(2,1)} async-done(((bf16[8,96,2560]{2,1,0:T(8,128)(2,1)}), bf16[8,96,2560]{2,1,0:T(8,128)(2,1)}, u32[]{:S(2)}, u32[]{:S(2)}) %all-to-all-start) | async-done | bytes 3932192 | tf_op jit(solution)/shard_map/all_to_all | solution.py:103
  65.1 5.5 %fusion.66 = (bf16[768,336]{0,1:T(8,128)(2,1)}, f32[768,336]{0,1:T(8,128)}) fusion(bf16[768,2560]{1,0:T(8,128)(2,1)} %bitcast, bf16[2560,336]{0,1:T(8,128)(2,1)} %param.16), kind=kOutput, calls=%fused_computation.144 | convolution fusion | flops 1321463808 | bytes 7200768 | tf_op jit(solution)/shard_map/dot_general | solution.py:106
  70.6 7.9 %convolution_convert_fusion.1 = bf16[768,1280]{1,0:T(8,128)(2,1)} fusion(bf16[768,2560]{1,0:T(8,128)(2,1)} %bitcast, bf16[2560,1280]{1,0:T(8,128)(2,1)S(1)} %bitcast.169), kind=kOutput, calls=%fused_computation.9 | convolution fusion | flops 5034147840 | bytes 12451840 | tf_op jit(solution)/shard_map/dot_general | solution.py:105
  78.5 2.1 copy.111
  80.6 1.5 pad_maximum_fusion.2
  82.2 0.1 copy-done.5
  82.3 1.2 pad_maximum_fusion.1
  83.5 1.0 slice.213
  84.5 0.1 broadcast_multiply_fusion
  84.7 1.7 reduce-window.6
  86.4 0.2 slice_reduce_fusion
  86.8 0.1 copy.121
  87.1 2.0 collective-permute-start
  89.1 0.6 bitcast_exponential_fusion
  89.8 0.7 copy.124
  90.5 0.6 copy.123
  91.1 0.7 copy.125
  91.8 5.0 %multiply_convert_fusion.2 = bf16[768,896]{1,0:T(8,128)(2,1)S(1)} fusion(bf16[768,896]{1,0:T(8,128)(2,1)} %pad_maximum_fusion.1, bf16[3,896]{1,0:T(4,128)(2,1)S(1)} %collective-permute-done, f32[896]{0:T(1024)S(1)} %get-tuple-element.6, f32[896]{0:T(1024)S(1)} %get-tuple-element.7, f32[896]{0:T(1024)S(1)} %get-tuple-element.8, f32[896]{0:T(1024)S(1)} %get-tuple-element.5, ...), kind=kLoop, calls=%fused_computation.10 | loop fusion | flops 17891328 | bytes 2775808 | tf_op jit(solution)/shard_map/convert_element_type | solution.py:124
  96.8 0.7 fusion.65
  97.5 1.1 slice.210
  98.5 2.3 copy.112
  100.8 3.8 %reshape.243 = bf16[3,256,10,64]{1,0,3,2:T(4,128)(2,1)} reshape(bf16[768,640]{0,1:T(8,128)(2,1)} %copy.112) | data formatting | bytes 1966080 | tf_op jit(solution)/shard_map/reshape | solution.py:126
  104.6 1.8 fusion.19
  106.4 2.8 %convolution_bitcast_fusion = f32[4,10,64,128]{3,0,2,1:T(4,128)S(1)} fusion(f32[3,10,64,128]{3,2,1,0:T(8,128)S(1)} %fusion.19, f32[10,3]{1,0:T(8,128)S(1)} %copy-done.15, f32[10,4]{1,0:T(8,128)S(1)} %copy-done.14, pred[4,3]{1,0:T(4,128)(4,1)S(1)} %copy-done.28), kind=kOutput, calls=%fused_computation.26 | convolution fusion | flops 11796840 | bytes 2294052 | tf_op jit(solution)/shard_map/hce,ehpn->chpn/dot_general | solution.py:162
  109.2 1.1 copy-done.2
  110.3 0.3 slice.387
  110.7 0.7 copy.128
  111.4 0.6 iota_compare_fusion
  112.0 1.4 slice_exponential_fusion
  113.4 13.8 %all-gather = bf16[8,1,10]{2,1,0:T(2,128)(2,1)S(1)} all-gather(bf16[1,1,10]{2,1,0:T(2,128)(2,1)S(1)} %slice_bitcast_fusion.5), channel_id=1, replica_groups=mesh['seq_0'=4,'seq_1'=8,'head'=8] {'seq_1'}, dimensions={0}, use_global_device_ids=true | all-gather | bytes 180 | tf_op jit(solution)/shard_map/all_gather | solution.py:31
  127.2 0.6 fusion.39
  127.8 0.6 convert_bitcast_fusion
  128.4 8.8 %all-gather.1 = bf16[4,1,10]{2,1,0:T(2,128)(2,1)} all-gather(bf16[1,1,10]{2,1,0:T(2,128)(2,1)S(1)} %get-tuple-element.17), channel_id=1, replica_groups=mesh['seq_0'=4,'seq_1'=8,'head'=8] {'seq_0'}, dimensions={0}, use_global_device_ids=true | all-gather | bytes 100 | tf_op jit(solution)/shard_map/all_gather | solution.py:31
  137.1 0.6 copy.115
  137.8 0.8 copy.127
  138.6 1.4 copy.119
  140.0 0.6 copy.117
  140.6 0.6 exponential_bitcast_fusion
  141.2 0.7 fusion.49
  141.9 2.1 fusion.67
  144.0 3.5 %all-gather.4.cloned.1.call-done = bf16[8,10,64,128]{3,2,1,0:T(8,128)(2,1)} async-done(((bf16[1,10,64,128]{3,2,1,0:T(8,128)(2,1)}), bf16[8,10,64,128]{3,2,1,0:T(8,128)(2,1)}) %all-gather.4.cloned.1.call-update) | async-done | bytes 1310736 | tf_op jit(solution)/shard_map/all_gather | solution.py:31
  147.5 1.9 fusion.28
  149.4 10.7 %all_gather.19 = bf16[4,10,64,128]{3,2,1,0:T(8,128)(2,1)S(1)} all-gather(bf16[1,10,64,128]{3,2,1,0:T(8,128)(2,1)S(1)} %fusion.28), channel_id=1, replica_groups=mesh['seq_0'=4,'seq_1'=8,'head'=8] {'seq_0'}, dimensions={0}, use_global_device_ids=true | all-gather | bytes 819200 | tf_op jit(solution)/shard_map/all_gather | solution.py:31
  160.2 1.0 add_bitcast_fusion
  161.1 0.4 slice_add_fusion
  161.6 0.9 fusion.21
  162.6 0.3 copy-done.7
  162.9 0.2 copy-done.8
  163.1 2.7 %fusion.8 = f32[3,256,10,64]{1,3,2,0:T(8,128)S(1)} fusion(f32[3,256,10,64]{1,3,2,0:T(8,128)S(1)} %fusion.21, f32[3,10,256]{2,1,0:T(8,128)S(1)} %copy-done.12, f32[3,10,256]{2,1,0:T(8,128)S(1)} %copy-done.10, f32[3,256,256]{2,1,0:T(8,128)S(1)} %copy-done.8, pred[256,256]{1,0:T(8,128)(4,1)S(1)} %copy-done.9, f32[10]{0:T(128)S(1)} %copy-done.31, ...), kind=kOutput, calls=%fused_computation.16 | convolution fusion | flops 265912320 | bytes 5859368 | tf_op jit(solution)/shard_map/chts,cshp->cthp/dot_general | solution.py:144
  165.8 1.4 copy.130
  167.2 1.8 copy.138
  168.9 2.8 %copy.131 = f32[768,640]{1,0:T(8,128)} copy(f32[768,640]{0,1:T(8,128)} %bitcast.167) | data formatting | bytes 3932160 | tf_op jit(solution)/shard_map/reshape | solution.py:188
  171.8 2.5 multiply_reduce_fusion
  174.3 17.4 %all_to_all.16 = f32[8,1,768]{2,1,0:T(1,128)S(1)} all-to-all(f32[8,1,768]{2,1,0:T(1,128)S(1)} %broadcast_in_dim.36), channel_id=1, replica_groups=mesh['seq_0'=4,'seq_1'=8,'head'=8] {'head'}, dimensions={0} | all-to-all | bytes 49152 | tf_op jit(solution)/shard_map/all_to_all | solution.py:48
  191.8 6.2 %convolution_convert_fusion = bf16[768,2560]{1,0:T(8,128)(2,1)S(1)} fusion(bf16[640,2560]{1,0:T(8,128)(2,1)S(1)} %copy-done, f32[640]{0:T(1024)S(1)} %copy-done.29, f32[768]{0:T(1024)S(1)} %add_rsqrt_fusion, f32[768,640]{1,0:T(8,128)} %copy.131, bf16[768,1280]{1,0:T(8,128)(2,1)} %convolution_convert_fusion.1), kind=kOutput, calls=%fused_computation.1 | convolution fusion | flops 2522972160 | bytes 10163712 | tf_op jit(solution)/shard_map/dot_general | solution.py:196
  197.9 49.8 %all_to_all.17 = bf16[8,96,2560]{2,1,0:T(8,128)(2,1)} all-to-all(bf16[8,96,2560]{2,1,0:T(8,128)(2,1)S(1)} %bitcast.170), channel_id=1, replica_groups=mesh['seq_0'=4,'seq_1'=8,'head'=8] {'head'}, dimensions={0} | all-to-all | bytes 7864320 | tf_op jit(solution)/shard_map/all_to_all | solution.py:65
  247.7 3.6 %reduce_sum.42 = bf16[96,2560]{1,0:T(8,128)(2,1)} reduce(bf16[8,96,2560]{2,1,0:T(8,128)(2,1)} %all_to_all.17, bf16[]{:T(256)} %constant.60.clone.1), dimensions={0}, to_apply=%region_6.7 | reduce | flops 1720320 | bytes 4423682 | tf_op jit(solution)/shard_map/reduce_sum | solution.py:66
  (86 shorter events, 0.8 us)
Async XLA Ops:
  6.5 185.2 %copy-start = (bf16[640,2560]{1,0:T(8,128)(2,1)S(1)}, bf16[640,2560]{1,0:T(8,128)(2,1)}, u32[]{:S(2)}) copy-start(bf16[640,2560]{1,0:T(8,128)(2,1)} %param.25) | copy-start | bytes 9830404
  11.5 53.6 %all-to-all-start = ((bf16[8,96,2560]{2,1,0:T(8,128)(2,1)}), bf16[8,96,2560]{2,1,0:T(8,128)(2,1)}, u32[]{:S(2)}, u32[]{:S(2)}) async-start(bf16[8,96,2560]{2,1,0:T(8,128)(2,1)} %stack.2), calls=%async_computation | async-start | bytes 7864320 | tf_op jit(solution)/shard_map/all_to_all | solution.py:103
  19.1 128.5 %all-gather.4.cloned.1.call-start = ((), (), s32[]{:S(2)}) async-start(), calls=%async_computation.3 | async-start | bytes 1474560 | tf_op jit(solution)/shard_map/all_gather | solution.py:31
  19.1 7.3 %copy-start.17 = (f32[4,640]{1,0:T(4,128)S(1)}, f32[4,640]{1,0:T(4,128)}, u32[]{:S(2)}) copy-start(f32[4,640]{1,0:T(4,128)} %param.17) | copy-start | bytes 30724
  19.1 7.3 %copy-start.23 = (f32[4,256]{1,0:T(4,128)S(1)}, f32[4,256]{1,0:T(4,128)}, u32[]{:S(2)}) copy-start(f32[4,256]{1,0:T(4,128)} %param.18) | copy-start | bytes 12292
  19.1 7.3 %copy-start.24 = (f32[640]{0:T(1024)S(1)}, f32[640]{0:T(1024)}, u32[]{:S(2)}) copy-start(f32[640]{0:T(1024)} %param.19) | copy-start | bytes 7684
  19.1 7.3 %copy-start.26 = (f32[256]{0:T(256)S(1)}, f32[256]{0:T(256)}, u32[]{:S(2)}) copy-start(f32[256]{0:T(256)} %param.20) | copy-start | bytes 3076
  19.1 7.9 %copy-start.30 = (f32[10]{0:T(128)S(1)}, f32[10]{0:T(128)}, u32[]{:S(2)}) copy-start(f32[10]{0:T(128)} %param.22) | copy-start | bytes 124
  65.1 5.5 %copy-start.4 = (bf16[320,8,2,640]{3,1,2,0:T(8,128)(2,1)S(1)}, bf16[320,8,2,640]{3,1,2,0:T(8,128)(2,1)}, u32[]{:S(2)}) copy-start(bf16[320,8,2,640]{3,1,2,0:T(8,128)(2,1)} %copy.137) | copy-start | bytes 19660804
  80.6 1.6 copy-start.1
  80.6 1.7 copy-start.5
  82.3 2.2 copy-start.27
  87.1 4.7 %copy-start.16 = (f32[3,10]{1,0:T(4,128)}, f32[3,10]{1,0:T(4,128)S(1)}, u32[]{:S(2)}) copy-start(f32[3,10]{1,0:T(4,128)S(1)} %reduce_window_sum.36) | copy-start | bytes 364
  87.1 4.7 %collective-permute-start = (bf16[3,896]{1,0:T(4,128)(2,1)}, bf16[3,896]{1,0:T(4,128)(2,1)S(1)}, u32[]{:S(2)}, u32[]{:S(2)}) collective-permute-start(bf16[3,896]{1,0:T(4,128)(2,1)} %pad_maximum_fusion.2), channel_id=1, source_target_pairs={{0,8},{8,16},{16,24},{24,32},{32,40},{40,48},{48,56},{56,64},{64,7... | collective-permute-start | bytes 16136 | tf_op jit(solution)/shard_map/ppermute | solution.py:16
  104.5 1.8 copy-start.14
  104.6 1.8 copy-start.15
  104.6 1.8 copy-start.28
  109.2 1.1 copy-start.2
  127.2 10.6 %copy-start.13 = (bf16[8,1,10]{2,1,0:T(2,128)(2,1)}, bf16[8,1,10]{2,1,0:T(2,128)(2,1)S(1)}, u32[]{:S(2)}) copy-start(bf16[8,1,10]{2,1,0:T(2,128)(2,1)S(1)} %all-gather) | copy-start | bytes 484
  137.8 22.3 %copy-start.18 = (f32[10]{0:T(128)S(1)}, f32[10]{0:T(128)}, u32[]{:S(2)}) copy-start(f32[10]{0:T(128)} %get-tuple-element.18) | copy-start | bytes 124
  137.8 22.3 %copy-start.19 = (f32[10]{0:T(128)S(1)}, f32[10]{0:T(128)}, u32[]{:S(2)}) copy-start(f32[10]{0:T(128)} %get-tuple-element.19) | copy-start | bytes 124
  137.8 22.3 %copy-start.20 = (f32[10]{0:T(128)S(1)}, f32[10]{0:T(128)}, u32[]{:S(2)}) copy-start(f32[10]{0:T(128)} %get-tuple-element.20) | copy-start | bytes 124
  137.8 22.3 %copy-start.21 = (f32[10]{0:T(128)S(1)}, f32[10]{0:T(128)}, u32[]{:S(2)}) copy-start(f32[10]{0:T(128)} %get-tuple-element.21) | copy-start | bytes 124
  137.8 22.3 %copy-start.22 = (f32[10]{0:T(128)S(1)}, f32[10]{0:T(128)}, u32[]{:S(2)}) copy-start(f32[10]{0:T(128)} %get-tuple-element.22) | copy-start | bytes 124
  140.6 19.5 %copy-start.25 = (f32[10]{0:T(128)S(1)}, f32[10]{0:T(128)}, u32[]{:S(2)}) copy-start(f32[10]{0:T(128)} %get-tuple-element.9) | copy-start | bytes 124
  147.5 12.6 %copy-start.6 = (bf16[8,10,64,128]{3,2,1,0:T(8,128)(2,1)S(1)}, bf16[8,10,64,128]{3,2,1,0:T(8,128)(2,1)}, u32[]{:S(2)}) copy-start(bf16[8,10,64,128]{3,2,1,0:T(8,128)(2,1)} %all-gather.4.cloned.1.call-done) | copy-start | bytes 3932164
  147.5 13.6 %copy-start.3 = (f32[4,10,64,128]{3,0,2,1:T(4,128)S(1)}, f32[4,10,64,128]{3,0,2,1:T(4,128)}, u32[]{:S(2)}) copy-start(f32[4,10,64,128]{3,0,2,1:T(4,128)} %copy-done.2) | copy-start | bytes 3932164
  161.6 1.3 copy-start.7
  161.6 1.5 copy-start.8
  161.6 1.5 copy-start.9
  161.6 1.5 copy-start.10
  161.6 1.5 copy-start.11
  161.6 1.5 copy-start.12
  161.6 1.5 copy-start.31
  171.8 20.0 %copy-start.29 = (f32[640]{0:T(1024)S(1)}, f32[640]{0:T(1024)}, u32[]{:S(2)}) copy-start(f32[640]{0:T(1024)} %param.24) | copy-start | bytes 7684
Sparse Core Ops, SparseCore 0:
  111.5 35.9 all-gather.3
